TPU v7x, 32 devices: a whole 2x2x4 slice. The times are simulated.
32 devices in a mesh: groups: 2 (over y), sky: 4 (over z), epoch: 2 (over x), band: 2 (over core).
Axes of the slice: x: 2, y: 2, z: 4, core: 2. Of those that a mesh axis runs over, the one named last changes fastest.
Arguments:
- slot_pixels: bfloat16 [96, 6, 32, 512], P(('groups', 'sky', 'epoch'), 'band'), parts along dimension 0, may hold values from -6 to 6
- slot_tile: int32 [96, 1], P(('groups', 'sky', 'epoch')), parts along dimension 0, may hold values from 0 to 3; in each aligned block of 6 rows (0 to 5, 6 to 11, ...) at most 2 rows name the same one
- slot_offset: int32 [96, 2], P(('groups', 'sky', 'epoch')), parts along dimension 0, may hold values from -5 to 5
- slot_frac: bfloat16 [96, 2], P(('groups', 'sky', 'epoch')), parts along dimension 0, may hold values from 0.049804688 to 0.94921875
- slot_sigma: bfloat16 [96, 6], P(('groups', 'sky', 'epoch'), 'band'), parts along dimension 0, may hold values from 0.5 to 2
- clip_mask: int32 [96, 6, 16], P(('groups', 'sky', 'epoch')), parts along dimension 0, may hold values 0 or 1
- slot_count: int32 [16], P(('groups', 'sky', 'epoch')), parts along dimension 0, may hold values from 4 to 6
- template: bfloat16 [6, 256, 512], P('band', ('groups', 'sky')), parts along dimension 1, may hold values from -6 to 6
- prior_weight: float32 [6, 256], P('band', ('groups', 'sky')), parts along dimension 1, may hold values from 0.5 to 4
Outputs:
- coadd_image: bfloat16 [6, 256, 512], P('band', ('groups', 'sky'), 'epoch'), parts along dimension 1
- depth_norm: bfloat16 [6, 256, 512], P('band', ('groups', 'sky'), 'epoch'), parts along dimension 1
There are 2 independent parts, one for each index of `groups`. A program takes and returns all parts, laid end to end along the dimension named above; each array names one. Nothing has to cross between parts.
Inputs may be any that keep to these rules, and one draw needn't show every extreme that they name: `slot_tile`: among the 6 rows of one reading device no owner is named more than 2 times, a bound that some block reaches. `slot_count`: slots of a reading device at or after its count are padding.
All inputs are finite; a program needn't handle non-finite values. No bound on the sum of `clip_mask` on one device may be relied on, other than what follows from the above.
Results may differ from a plain program's by a relative error of at most 0.014.
Values may be sent and summed in bfloat16 or wider, within the bound.
A program may use at most 64 MiB of HBM per device.

v0:
```python
import math

import jax
import jax.numpy as jnp
from jax import lax
from jax.sharding import PartitionSpec as P

ROWS_DEV = 32
MARGIN = 8
CAPACITY = 2


CLIP_WIDTH = 3.0


def padded(cells, sides, width):
    for axis, dim in sides:
        count = lax.axis_size(axis)
        ends = count - 1
        head = lax.slice_in_dim(cells, 0, width, axis=dim)
        tail = lax.slice_in_dim(cells, cells.shape[dim] - width, cells.shape[dim], axis=dim)
        cells = jnp.concatenate(
            [
                lax.ppermute(tail, axis, [(i, (i + 1) % count) for i in range(ends)]),
                cells,
                lax.ppermute(head, axis, [((i + 1) % count, i) for i in range(ends)]),
            ],
            axis=dim,
        )
    return cells


def lanczos(distance):
    inside = jnp.abs(distance) < 3.0
    return jnp.where(inside, jnp.sinc(distance) * jnp.sinc(distance / 3.0), 0.0)


def warp_table(shifts, fractions, length_out, length_in, margin_rows):
    out_index = lax.broadcasted_iota(jnp.int32, (1, length_out, length_in), 1)
    in_index = lax.broadcasted_iota(jnp.int32, (1, length_out, length_in), 2)
    gap_index = out_index - margin_rows - shifts[:, None, None] - in_index
    distance = gap_index.astype(jnp.float32) - fractions[:, None, None]
    return lanczos(distance).astype(jnp.bfloat16)


def warp_columns(pixels, shifts, fractions):
    tile_cols = pixels.shape[3]
    kernel_table = warp_table(shifts, fractions, tile_cols, tile_cols, 0)
    warped = jnp.einsum("sbrk,sjk->sbrj", pixels, kernel_table, preferred_element_type=jnp.float32)
    return warped.astype(jnp.bfloat16)


def column_cover(shifts, fractions, tile_cols):
    column_index = lax.broadcasted_iota(jnp.int32, (1, tile_cols), 1)
    cover = jnp.zeros((shifts.shape[0], tile_cols), jnp.float32)
    for step_back in range(-3, 3):
        rounded = lanczos(jnp.float32(-step_back) - fractions).astype(jnp.bfloat16)
        weight_tap = lax.optimization_barrier(rounded).astype(jnp.float32)
        source_col = column_index - shifts[:, None] + step_back
        inside = (source_col >= 0) & (source_col < tile_cols)
        cover = cover + jnp.where(inside, weight_tap[:, None], 0.0)
    return jnp.clip(cover, 0.0, 1.0)


def epoch_sum(totals):
    return lax.psum_scatter(
        totals.astype(jnp.bfloat16), "epoch", scatter_dimension=3, tiled=True
    ).astype(jnp.float32)


def add_seams(totals):
    rims = jnp.concatenate([totals[:, :, :MARGIN], totals[:, :, -MARGIN:]], 2)
    framed_rims = padded(rims.astype(jnp.bfloat16), (("sky", 2),), MARGIN).astype(rims.dtype)
    own_rows = totals[:, :, MARGIN : MARGIN + ROWS_DEV]
    own_rows = own_rows.at[:, :, :MARGIN].add(framed_rims[:, :, :MARGIN])
    own_rows = own_rows.at[:, :, ROWS_DEV - MARGIN :].add(framed_rims[:, :, 3 * MARGIN :])
    return own_rows


def on_device(
    slot_pixels,
    slot_tile,
    slot_offset,
    slot_frac,
    slot_sigma,
    clip_mask,
    slot_count,
    template,
    prior_weight,
):
    sky_count = lax.axis_size("sky")
    held = slot_pixels.shape[0]
    tile_cols = slot_pixels.shape[3]
    local_bands = slot_pixels.shape[1]
    canvas_rows = ROWS_DEV + 2 * MARGIN
    routes_total = sky_count * CAPACITY
    target = slot_tile[:, 0]
    owners = jnp.arange(sky_count, dtype=jnp.int32)
    onehot = (target[:, None] == owners[None, :]).astype(jnp.int32)
    slot_rank = jnp.sum(jnp.cumsum(onehot, 0) * onehot, 1) - 1
    position = target * CAPACITY + slot_rank
    held_index = jnp.arange(held, dtype=jnp.int32)
    is_live = held_index < slot_count[0]
    chooser = position[None, :] == jnp.arange(routes_total, dtype=jnp.int32)[:, None]
    source = jnp.sum(jnp.where(chooser, held_index[None, :], 0), 1)
    filled = jnp.any(chooser & is_live[None, :], 1).astype(jnp.int32)

    def pack(array):
        taken = jnp.take(array, source, axis=0)
        return taken.reshape((sky_count, CAPACITY) + array.shape[1:])

    packed_mask = pack(clip_mask) * filled.reshape(sky_count, CAPACITY)[:, :, None, None]
    received = (
        lax.all_to_all(pack(slot_pixels), "sky", split_axis=0, concat_axis=0, tiled=True),
        lax.all_to_all(pack(slot_offset), "sky", split_axis=0, concat_axis=0, tiled=True),
        lax.all_to_all(pack(slot_frac), "sky", split_axis=0, concat_axis=0, tiled=True),
        lax.all_to_all(pack(slot_sigma), "sky", split_axis=0, concat_axis=0, tiled=True),
        lax.all_to_all(packed_mask, "sky", split_axis=0, concat_axis=0, tiled=True),
    )
    received = tuple((array.reshape((routes_total,) + array.shape[2:]) for array in received))
    framed = padded(template, (("sky", 1),), MARGIN).astype(jnp.float32)

    def accumulate(totals, pieces):
        pixels, offsets, fractions, sigmas, masks = pieces
        fractions = fractions.astype(jnp.float32)
        columns = warp_columns(pixels, offsets[:, 1], fractions[:, 1])
        row_table = warp_table(offsets[:, 0], fractions[:, 0], canvas_rows, ROWS_DEV, MARGIN)
        warped = jnp.einsum(
            "sir,sbrj->sbij", row_table, columns, preferred_element_type=jnp.float32
        )
        row_cover = jnp.clip(jnp.sum(row_table.astype(jnp.float32), 2), 0.0, 1.0)
        col_cover = column_cover(offsets[:, 1], fractions[:, 1], tile_cols)
        block_slots = masks.shape[0]
        block_mask = masks.astype(jnp.float32)
        expanded = jnp.broadcast_to(
            block_mask[:, :, None, :, None], (block_slots, canvas_rows // 8, 8, tile_cols // 32, 32)
        )
        expanded = expanded.reshape(block_slots, canvas_rows, tile_cols)
        plane = expanded * row_cover[:, :, None] * col_cover[:, None, :]
        sigma_values = sigmas.astype(jnp.float32)
        weight = plane[:, None] / (sigma_values * sigma_values)[:, :, None, None]
        scale = CLIP_WIDTH * sigma_values[:, :, None, None]
        clipped = framed[None] + scale * jnp.tanh((warped - framed[None]) / scale)
        flux_part = jnp.sum(weight * clipped, 0)
        weight_part = jnp.sum(weight, 0)
        return (totals + jnp.stack([flux_part, weight_part], 0), None)

    block_slots = math.gcd(8, routes_total)
    blocked = tuple(
        (
            array.reshape((routes_total // block_slots, block_slots) + array.shape[1:])
            for array in received
        )
    )
    initial = jnp.zeros((2, local_bands, canvas_rows, tile_cols), jnp.float32)
    totals, _ = lax.scan(accumulate, initial, blocked)
    own_rows = add_seams(epoch_sum(totals))
    flux_sum = own_rows[0]
    weight_sum = own_rows[1]
    part_width = own_rows.shape[3]
    epoch_position = lax.axis_index("epoch")
    template_part = lax.dynamic_slice_in_dim(
        template, epoch_position * part_width, part_width, 2
    ).astype(jnp.float32)
    prior = prior_weight[:, :, None]
    coadd_image = ((flux_sum + prior * template_part) / (weight_sum + prior)).astype(jnp.bfloat16)
    depth_map = weight_sum + prior
    band_total = lax.psum(jnp.sum(depth_map, axis=(1, 2)), ("sky", "epoch"))
    band_mean = band_total / (ROWS_DEV * sky_count * tile_cols)
    depth_norm = (depth_map / band_mean[:, None, None]).astype(jnp.bfloat16)
    return (coadd_image, depth_norm)


def solution(mesh):
    in_specs = (
        P(("groups", "sky", "epoch"), "band", None, None),
        P(("groups", "sky", "epoch"), None),
        P(("groups", "sky", "epoch"), None),
        P(("groups", "sky", "epoch"), None),
        P(("groups", "sky", "epoch"), "band"),
        P(("groups", "sky", "epoch"), None, None),
        P(("groups", "sky", "epoch")),
        P("band", ("groups", "sky"), None),
        P("band", ("groups", "sky")),
    )
    out_specs = (P("band", ("groups", "sky"), "epoch"), P("band", ("groups", "sky"), "epoch"))
    return jax.shard_map(
        on_device, mesh=mesh, in_specs=in_specs, out_specs=out_specs, check_vma=False
    )
```

profile of v0, /device:TPU:0, one launch (start us, length us, event | category | flops | bytes accessed | tf_op | source)
XLA Modules:
  0.0 150.9 jit_solution(16778210866701196736)
XLA Ops:
  7.2 0.7 fusion.117
  7.9 0.2 reduce_window_sum.11
  8.1 0.7 select_reduce_fusion.1
  8.8 0.7 add_add_fusion
  9.6 0.8 copy.65
  10.4 0.6 gather_fusion.2
  11.0 0.1 copy.74
  11.1 0.6 copy.67
  11.7 6.3 %all-to-all-start.2 = ((bf16[4,2,2]{1,2,0:T(2,128)(2,1)}), bf16[4,2,2]{1,2,0:T(2,128)(2,1)S(1)}, u32[]{:S(2)}, u32[]{:S(2)}) async-start(bf16[4,2,2]{1,2,0:T(2,128)(2,1)} %copy.67), calls=%async_computation.2 | async-start | bytes 4096 | tf_op jit(solution)/shard_map/all_to_all | solution.py:116
  18.0 0.8 fusion.206
  18.8 1.3 collective-permute-start.1
  20.1 4.6 %collective-permute-start = (bf16[3,8,512]{2,1,0:T(8,128)(2,1)S(1)}, bf16[3,8,512]{2,1,0:T(8,128)(2,1)S(1)}, u32[]{:S(2)}, u32[]{:S(2)}) collective-permute-start(bf16[3,8,512]{2,1,0:T(8,128)(2,1)S(1)} %get-tuple-element.57), channel_id=1, source_target_pairs={{0,4},{4,8},{8,12},{1,5},{5,9},{9,13},{2,6},{6,10},{10,14},{3,7},{... | collective-permute-start | bytes 73736 | tf_op jit(solution)/shard_map/ppermute | solution.py:24
  24.7 0.8 copy.70
  25.4 0.6 gather_fusion.3
  26.0 0.7 broadcast_select_fusion.1
  26.7 1.3 gather_fusion
  29.0 0.7 reshape.370
  29.6 0.8 copy.61
  30.4 0.6 gather_fusion.1
  31.1 0.6 copy.63
  31.7 0.6 gather_fusion.4
  32.3 1.0 broadcast_select_fusion
  33.3 4.2 %all-to-all-start.3 = ((bf16[4,2,3]{2,1,0:T(2,128)(2,1)}), bf16[4,2,3]{2,1,0:T(2,128)(2,1)S(1)}, u32[]{:S(2)}, u32[]{:S(2)}) async-start(bf16[4,2,3]{2,1,0:T(2,128)(2,1)} %broadcast_select_fusion.1), calls=%async_computation.3 | async-start | bytes 4096 | tf_op jit(solution)/shard_map/all_to_all | solution.py:117
  38.0 5.0 %all-to-all-done.3 = bf16[4,2,3]{2,1,0:T(2,128)(2,1)S(1)} async-done(((bf16[4,2,3]{2,1,0:T(2,128)(2,1)}), bf16[4,2,3]{2,1,0:T(2,128)(2,1)S(1)}, u32[]{:S(2)}, u32[]{:S(2)}) %all-to-all-start.3) | async-done | bytes 80 | tf_op jit(solution)/shard_map/all_to_all | solution.py:117
  42.9 3.2 %all-to-all-start.1 = ((s32[4,2,2]{1,2,0:T(2,128)}), s32[4,2,2]{1,2,0:T(2,128)S(1)}, u32[]{:S(2)}, u32[]{:S(2)}) async-start(s32[4,2,2]{1,2,0:T(2,128)} %copy.63), calls=%async_computation.1 | async-start | bytes 8192 | tf_op jit(solution)/shard_map/all_to_all | solution.py:115
  46.2 5.5 %all-to-all-done.1 = s32[4,2,2]{1,2,0:T(2,128)S(1)} async-done(((s32[4,2,2]{1,2,0:T(2,128)}), s32[4,2,2]{1,2,0:T(2,128)S(1)}, u32[]{:S(2)}, u32[]{:S(2)}) %all-to-all-start.1) | async-done | bytes 96 | tf_op jit(solution)/shard_map/all_to_all | solution.py:115
  51.7 3.2 %all-to-all-start = ((s32[4,1,192]{2,1,0:T(1,128)}), s32[4,1,192]{2,1,0:T(1,128)S(1)}, u32[]{:S(2)}, u32[]{:S(2)}) async-start(s32[4,1,192]{2,1,0:T(1,128)} %reshape.370), calls=%async_computation | async-start | bytes 8192 | tf_op jit(solution)/shard_map/all_to_all | solution.py:118
  55.1 0.4 convert_reduce_fusion
  55.5 5.0 %all-to-all-done = s32[4,1,192]{2,1,0:T(1,128)S(1)} async-done(((s32[4,1,192]{2,1,0:T(1,128)}), s32[4,1,192]{2,1,0:T(1,128)S(1)}, u32[]{:S(2)}, u32[]{:S(2)}) %all-to-all-start) | async-done | bytes 3104 | tf_op jit(solution)/shard_map/all_to_all | solution.py:118
  60.5 3.5 %all-to-all-start.4 = ((bf16[4,2,3,32,512]{4,3,2,1,0:T(8,128)(2,1)}), bf16[4,2,3,32,512]{4,3,2,1,0:T(8,128)(2,1)S(1)}, u32[]{:S(2)}, u32[]{:S(2)}) async-start(bf16[4,2,3,32,512]{4,3,2,1,0:T(8,128)(2,1)} %broadcast_select_fusion), calls=%async_computation.4 | async-start | bytes 1572864 | tf_op jit(solution)/shard_map/all_to_all | solution.py:114
  64.2 0.5 broadcast.884
  64.7 0.7 reduce.4
  65.5 1.9 %broadcast_in_dim.182 = f32[8,6,8,16,32]{4,3,2,1,0:T(8,128)} broadcast(f32[8,6,16]{2,1,0:T(8,128)S(1)} %copy.60), dimensions={0,1,3} | broadcast | bytes 789504 | tf_op jit(solution)/shard_map/while/body/eval_jaxpr/broadcast_in_dim | solution.py:135
  67.5 2.9 %reshape.325 = f32[8,48,512]{2,1,0:T(8,128)S(1)} reshape(f32[8,6,8,16,32]{4,3,2,1,0:T(8,128)} %broadcast_in_dim.182) | data formatting | bytes 1572864 | tf_op jit(solution)/shard_map/while/body/eval_jaxpr/reshape | solution.py:138
  70.3 0.1 multiply_multiply_fusion.8
  70.5 0.2 divide_reduce_fusion
  70.8 8.9 %all-to-all-done.4 = bf16[4,2,3,32,512]{4,3,2,1,0:T(8,128)(2,1)S(1)} async-done(((bf16[4,2,3,32,512]{4,3,2,1,0:T(8,128)(2,1)}), bf16[4,2,3,32,512]{4,3,2,1,0:T(8,128)(2,1)S(1)}, u32[]{:S(2)}, u32[]{:S(2)}) %all-to-all-start.4) | async-done | bytes 786464 | tf_op jit(solution)/shard_map/all_to_all | solution.py:114
  79.7 22.0 %fusion.41 = bf16[3,48,512]{2,1,0:T(8,128)(2,1)S(1)} fusion(f32[8,3]{1,0:T(8,128)S(1)} %bitcast.115, f32[3,48,512]{2,1,0:T(8,128)S(1)} %maximum_convert_fusion, f32[8,3]{1,0:T(8,128)S(1)} %bitcast.111, f32[8,48,512]{2,1,0:T(8,128)S(1)} %multiply_multiply_fusion.8, bf16[8,3,32,512]{3,2,1,0:T(8,128)(2,1)S(1)} %bitcast.104, f32[8]{0:T(128)S(1)} %get-tuple-element.61, ...), kind=kOutput, calls=%fused_computation.69 | convolution fusion | flops 603058176 | bytes 2015744 | tf_op jit(solution)/shard_map/while/body/eval_jaxpr/sir,sbrj->sbij/dot_general | solution.py:128
  101.7 0.7 pad_maximum_fusion
  102.4 11.4 %reduce-scatter.2.cloned.1.call-done = bf16[2,3,48,256]{3,2,1,0:T(8,128)(2,1)} async-done(((bf16[2,3,48,512]{3,2,1,0:T(8,128)(2,1)}), bf16[2,3,48,256]{3,2,1,0:T(8,128)(2,1)}) %reduce-scatter.2.cloned.1.call-update) | async-done | bytes 147472 | tf_op jit(solution)/shard_map/reduce_scatter | solution.py:66
  113.8 0.8 fusion.205
  114.6 1.3 collective-permute-start.3
  115.8 4.5 %collective-permute-start.2 = (bf16[2,3,8,256]{3,2,1,0:T(8,128)(2,1)S(1)}, bf16[2,3,8,256]{3,2,1,0:T(8,128)(2,1)S(1)}, u32[]{:S(2)}, u32[]{:S(2)}) collective-permute-start(bf16[2,3,8,256]{3,2,1,0:T(8,128)(2,1)S(1)} %get-tuple-element.55), channel_id=1, source_target_pairs={{0,4},{4,8},{8,12},{1,5},{5,9},{9,13},{2,6},{6,10},{10,14},{3,7},{... | collective-permute-start | bytes 73736 | tf_op jit(solution)/shard_map/ppermute | solution.py:24
  120.4 0.9 slice.133
  121.3 0.9 convert_element_type.175
  122.3 0.2 fusion.83
  122.5 20.9 %psum.7 = f32[3]{0:T(128)S(1)} all-reduce(f32[3]{0:T(128)S(1)} %fusion.83), channel_id=1, replica_groups=mesh['groups'=2,'sky'=4,'epoch'=2,'band'=2] {'sky','epoch'}, use_global_device_ids=true, to_apply=%region_9.13 | all-reduce | flops 3 | bytes 24 | tf_op jit(solution)/shard_map/psum | solution.py:168
  143.4 0.7 divide_convert_fusion
  (53 shorter events, 1.5 us)
Async XLA Ops:
  7.2 24.5 %copy-start = (bf16[6,3,32,512]{3,2,1,0:T(8,128)(2,1)S(1)}, bf16[6,3,32,512]{3,2,1,0:T(8,128)(2,1)}, u32[]{:S(2)}) copy-start(bf16[6,3,32,512]{3,2,1,0:T(8,128)(2,1)} %param.16) | copy-start | bytes 1769476
  11.7 21.6 %all-to-all-start.2 = ((bf16[4,2,2]{1,2,0:T(2,128)(2,1)}), bf16[4,2,2]{1,2,0:T(2,128)(2,1)S(1)}, u32[]{:S(2)}, u32[]{:S(2)}) async-start(bf16[4,2,2]{1,2,0:T(2,128)(2,1)} %copy.67), calls=%async_computation.2 | async-start | bytes 4096 | tf_op jit(solution)/shard_map/all_to_all | solution.py:116
  18.8 51.9 %collective-permute-start.1 = (bf16[3,8,512]{2,1,0:T(8,128)(2,1)S(1)}, bf16[3,8,512]{2,1,0:T(8,128)(2,1)S(1)}, u32[]{:S(2)}, u32[]{:S(2)}) collective-permute-start(bf16[3,8,512]{2,1,0:T(8,128)(2,1)S(1)} %get-tuple-element.58), channel_id=1, source_target_pairs={{4,0},{8,4},{12,8},{5,1},{9,5},{13,9},{6,2},{10,6},{14,10},{7,3},{... | collective-permute-start | bytes 73736 | tf_op jit(solution)/shard_map/ppermute | solution.py:26
  20.1 50.6 %collective-permute-start = (bf16[3,8,512]{2,1,0:T(8,128)(2,1)S(1)}, bf16[3,8,512]{2,1,0:T(8,128)(2,1)S(1)}, u32[]{:S(2)}, u32[]{:S(2)}) collective-permute-start(bf16[3,8,512]{2,1,0:T(8,128)(2,1)S(1)} %get-tuple-element.57), channel_id=1, source_target_pairs={{0,4},{4,8},{8,12},{1,5},{5,9},{9,13},{2,6},{6,10},{10,14},{3,7},{... | collective-permute-start | bytes 73736 | tf_op jit(solution)/shard_map/ppermute | solution.py:24
  33.3 9.6 %all-to-all-start.3 = ((bf16[4,2,3]{2,1,0:T(2,128)(2,1)}), bf16[4,2,3]{2,1,0:T(2,128)(2,1)S(1)}, u32[]{:S(2)}, u32[]{:S(2)}) async-start(bf16[4,2,3]{2,1,0:T(2,128)(2,1)} %broadcast_select_fusion.1), calls=%async_computation.3 | async-start | bytes 4096 | tf_op jit(solution)/shard_map/all_to_all | solution.py:117
  42.9 8.8 %all-to-all-start.1 = ((s32[4,2,2]{1,2,0:T(2,128)}), s32[4,2,2]{1,2,0:T(2,128)S(1)}, u32[]{:S(2)}, u32[]{:S(2)}) async-start(s32[4,2,2]{1,2,0:T(2,128)} %copy.63), calls=%async_computation.1 | async-start | bytes 8192 | tf_op jit(solution)/shard_map/all_to_all | solution.py:115
  51.7 8.8 %all-to-all-start = ((s32[4,1,192]{2,1,0:T(1,128)}), s32[4,1,192]{2,1,0:T(1,128)S(1)}, u32[]{:S(2)}, u32[]{:S(2)}) async-start(s32[4,1,192]{2,1,0:T(1,128)} %reshape.370), calls=%async_computation | async-start | bytes 8192 | tf_op jit(solution)/shard_map/all_to_all | solution.py:118
  60.5 19.2 %all-to-all-start.4 = ((bf16[4,2,3,32,512]{4,3,2,1,0:T(8,128)(2,1)}), bf16[4,2,3,32,512]{4,3,2,1,0:T(8,128)(2,1)S(1)}, u32[]{:S(2)}, u32[]{:S(2)}) async-start(bf16[4,2,3,32,512]{4,3,2,1,0:T(8,128)(2,1)} %broadcast_select_fusion), calls=%async_computation.4 | async-start | bytes 1572864 | tf_op jit(solution)/shard_map/all_to_all | solution.py:114
  64.0 49.8 %reduce-scatter.2.cloned.1.call-start = ((), (), s32[]{:S(2)}) async-start(), calls=%async_computation.6 | async-start | bytes 442368 | tf_op jit(solution)/shard_map/reduce_scatter | solution.py:66
  67.5 3.3 %copy-start.1 = (bf16[3,32,512]{2,1,0:T(8,128)(2,1)S(1)}, bf16[3,32,512]{2,1,0:T(8,128)(2,1)}, u32[]{:S(2)}) copy-start(bf16[3,32,512]{2,1,0:T(8,128)(2,1)} %param.23) | copy-start | bytes 294916
  79.7 42.6 %copy-start.2 = (f32[3,32]{1,0:T(4,128)S(1)}, f32[3,32]{1,0:T(4,128)}, u32[]{:S(2)}) copy-start(f32[3,32]{1,0:T(4,128)} %param.24) | copy-start | bytes 1156
  114.6 7.7 %collective-permute-start.3 = (bf16[2,3,8,256]{3,2,1,0:T(8,128)(2,1)S(1)}, bf16[2,3,8,256]{3,2,1,0:T(8,128)(2,1)S(1)}, u32[]{:S(2)}, u32[]{:S(2)}) collective-permute-start(bf16[2,3,8,256]{3,2,1,0:T(8,128)(2,1)S(1)} %get-tuple-element.56), channel_id=1, source_target_pairs={{4,0},{8,4},{12,8},{5,1},{9,5},{13,9},{6,2},{10,6},{14,10},{7,3},{... | collective-permute-start | bytes 73736 | tf_op jit(solution)/shard_map/ppermute | solution.py:26
  115.8 6.4 %collective-permute-start.2 = (bf16[2,3,8,256]{3,2,1,0:T(8,128)(2,1)S(1)}, bf16[2,3,8,256]{3,2,1,0:T(8,128)(2,1)S(1)}, u32[]{:S(2)}, u32[]{:S(2)}) collective-permute-start(bf16[2,3,8,256]{3,2,1,0:T(8,128)(2,1)S(1)} %get-tuple-element.55), channel_id=1, source_target_pairs={{0,4},{4,8},{8,12},{1,5},{5,9},{9,13},{2,6},{6,10},{10,14},{3,7},{... | collective-permute-start | bytes 73736 | tf_op jit(solution)/shard_map/ppermute | solution.py:24
Sparse Core Ops, SparseCore 0:
  102.5 11.2 reduce-scatter.1
where the time goes:
time: 152 us; the launch traced here: 151 us
  waiting for transfers between devices  35.8 us (24%)
  starting transfers between devices  32.2 us (21%)
  matrix products  22 us (14%)
  blocking collectives  20.9 us (14%)
  local copies, waits for them, and re-layouts  16.4 us (11%)
  between operations  15 us (10%)
  other arithmetic  8.59 us (6%)
    dot_general x1, matrix products, accumulate(): jnp.einsum('sir,sbrj->sbij', row_table, columns, preferred_element_type=j...  22 us
    psum x1, blocking collectives, on_device(): band_total = lax.psum(jnp.sum(depth_map, axis=(1, 2)), ('sky', 'epoch'))  20.9 us
    reduce_scatter x1, waiting for transfers between devices, epoch_sum(): lax.psum_scatter(totals.astype(jnp.bfloat16), 'epoch', scatter_dimension=...  11.4 us
    ppermute x2, starting transfers between devices, padded(): lax.ppermute(tail, axis, [(i, (i + 1) % count) for i in range(ends)])  9.1 us
    all_to_all x1, waiting for transfers between devices, on_device(): lax.all_to_all(pack(slot_pixels), 'sky', split_axis=0, concat_axis=0, til...  8.91 us
    all_to_all x1, starting transfers between devices, on_device(): lax.all_to_all(pack(slot_frac), 'sky', split_axis=0, concat_axis=0, tiled...  6.35 us
    all_to_all x1, waiting for transfers between devices, on_device(): lax.all_to_all(pack(slot_offset), 'sky', split_axis=0, concat_axis=0, til...  5.53 us
    all_to_all x1, waiting for transfers between devices, on_device(): lax.all_to_all(packed_mask, 'sky', split_axis=0, concat_axis=0, tiled=True)  5.02 us
  transfers between devices with their start and end apart: 10, of which 5 were waited for; matrix products, arithmetic and copies ran while one was open for 12% of the time, Pallas kernels for 0%

commit v1 on v0

v1 whole, which is shorter than its diff:
```python
import functools

import jax
import jax.numpy as jnp
from jax import lax
from jax.experimental import pallas as pl
from jax.experimental.pallas import tpu as pltpu
from jax.sharding import PartitionSpec as P

MARGIN = 8
BLOCK_ROWS = 8
REACH = 3
LANES = 128
CLIP_WIDTH = 3.0
MESH = pl.DeviceIdType.MESH


def lanczos(distance):
    inside = jnp.abs(distance) < 3.0
    return jnp.where(inside, jnp.sinc(distance) * jnp.sinc(distance / 3.0), 0.0)


def tap_weights(fractions):
    steps_back = jnp.arange(-REACH, REACH, dtype=jnp.int32)
    distance = (-steps_back).astype(jnp.float32) - fractions.astype(jnp.float32)[..., None]
    rounded = lanczos(distance).astype(jnp.bfloat16)
    return lax.optimization_barrier(rounded).astype(jnp.float32)


def gather_kernel(sky, own_ref, all_ref, held, send_sem, recv_sem):
    me = lax.axis_index("sky")
    barrier = pltpu.get_barrier_semaphore()
    for d in range(1, sky):
        pl.semaphore_signal(
            barrier, inc=1, device_id={"sky": lax.rem(me + d, sky)}, device_id_type=MESH
        )
    pl.semaphore_wait(barrier, sky - 1)
    copies = []
    for d in range(1, sky):
        copy = pltpu.make_async_remote_copy(
            src_ref=own_ref,
            dst_ref=held.at[d - 1],
            send_sem=send_sem.at[d - 1],
            recv_sem=recv_sem.at[d - 1],
            device_id={"sky": lax.rem(me + d, sky)},
            device_id_type=MESH,
        )
        copy.start()
        copies.append(copy)
    all_ref[me] = own_ref[...]
    for d in range(1, sky):
        copies[d - 1].wait()
        all_ref[lax.rem(me - d + sky, sky)] = held[d - 1]


def warp_kernel(
    bands, sky, epochs, rows,
    tile_ref, offset_ref, taps_ref, sigma_ref,
    pixels_ref, mask_ref, template_ref, prior_ref,
    send_ref, total_ref,
    framed, flux, weights, source, wide_mask,
):
    slots = pixels_ref.shape[0]
    cols = pixels_ref.shape[2]
    padded = cols + LANES
    canvas = rows + 2 * MARGIN
    blocks = canvas // BLOCK_ROWS
    part = cols // epochs
    mask_cols = mask_ref.shape[1]

    flux[...] = jnp.zeros_like(flux)
    weights[...] = jnp.zeros_like(weights)
    edge = jnp.zeros((bands, MARGIN, cols), jnp.float32)
    framed[:, :MARGIN] = edge
    framed[:, MARGIN + sky * rows :] = edge
    for s in range(sky):
        framed[:, MARGIN + s * rows : MARGIN + (s + 1) * rows] = template_ref[s].astype(jnp.float32)
    source[:, cols:] = jnp.zeros((source.shape[0], LANES), jnp.float32)
    source[bands * rows :, :cols] = jnp.ones((8, cols), jnp.float32)
    cell = lax.broadcasted_iota(jnp.int32, (mask_cols, cols), 0)
    column = lax.broadcasted_iota(jnp.int32, (mask_cols, cols), 1) // (cols // mask_cols)
    spread = jnp.where(cell == column, 1.0, 0.0).astype(jnp.bfloat16)
    wide_mask[...] = jnp.dot(
        mask_ref[...], spread, preferred_element_type=jnp.float32
    ).reshape(wide_mask.shape)
    gap = (
        lax.broadcasted_iota(jnp.int32, (canvas, rows), 0)
        - lax.broadcasted_iota(jnp.int32, (canvas, rows), 1)
        - MARGIN
    )

    def one_slot(p, carry):
        dy, dx = offset_ref[p, 0], offset_ref[p, 1]
        source[: bands * rows, :cols] = pixels_ref[p].astype(jnp.float32)
        base = pltpu.roll(source[...], lax.rem(dx + padded, padded), 1)
        summed = taps_ref[p, 2 * REACH + REACH] * base
        for tap in range(2 * REACH):
            if tap != REACH:
                moved = pltpu.roll(base, (REACH - tap) % padded, 1)
                summed = summed + taps_ref[p, 2 * REACH + tap] * moved
        columns = summed[: bands * rows, :cols].astype(jnp.bfloat16)
        col_cover = jnp.clip(summed[bands * rows :, :cols], 0.0, 1.0)
        row_table = jnp.zeros((canvas, rows), jnp.float32)
        for tap in range(2 * REACH):
            row_table = row_table + jnp.where(gap == dy + REACH - tap, taps_ref[p, tap], 0.0)
        row_cover = jnp.clip(jnp.sum(row_table, 1, keepdims=True), 0.0, 1.0)
        row_table = row_table.astype(jnp.bfloat16)
        pieces = []
        for i in range(blocks):
            cover = row_cover[i * BLOCK_ROWS : (i + 1) * BLOCK_ROWS]
            pieces.append(wide_mask[p, i : i + 1] * cover * col_cover)
        plane = jnp.concatenate(pieces, 0)
        start = pl.multiple_of(tile_ref[p] * rows, 8)
        for b in range(bands):
            warped = jnp.dot(
                row_table, columns[b * rows : (b + 1) * rows], preferred_element_type=jnp.float32
            )
            frame = framed[b, pl.ds(start, canvas)]
            scale = sigma_ref[p, b]
            clipped = frame + scale * jnp.tanh((warped - frame) * sigma_ref[p, bands + b])
            weight = plane * sigma_ref[p, 2 * bands + b]
            flux[b, pl.ds(start, canvas)] += weight * clipped
            weights[b, pl.ds(start, canvas)] += weight
        return carry

    lax.fori_loop(0, slots, one_slot, 0)
    for s in range(sky):
        near = slice(MARGIN + s * rows, MARGIN + (s + 1) * rows)
        for e in range(epochs):
            far = slice(e * part, (e + 1) * part)
            send_ref[s * epochs + e, 0] = flux[:, near, far].astype(jnp.bfloat16)
            send_ref[s * epochs + e, 1] = weights[:, near, far].astype(jnp.bfloat16)
    total_ref[...] = jnp.zeros_like(total_ref)
    for b in range(bands):
        along = jnp.sum(weights[b, MARGIN : MARGIN + sky * rows], 0, keepdims=True)
        folded = along[:, :LANES]
        for c in range(1, cols // LANES):
            folded = folded + along[:, c * LANES : (c + 1) * LANES]
        prior = jnp.sum(prior_ref[b], 0, keepdims=True)
        total_ref[b : b + 1] = folded + prior * (part / LANES)


def exchange_kernel(
    bands, sky, epochs, pixels_all,
    send_ref, total_ref, template_ref, prior_ref,
    coadd_ref, depth_ref,
    held, held_total, send_sem, recv_sem, send_total_sem, recv_total_sem,
):
    count = sky * epochs
    part = coadd_ref.shape[2]
    epoch = lax.axis_index("epoch")
    me = lax.axis_index("sky") * epochs + epoch

    def peer(d):
        index = lax.rem(me + d, count)
        return index, {"sky": index // epochs, "epoch": lax.rem(index, epochs)}

    barrier = pltpu.get_barrier_semaphore()
    for d in range(1, count):
        pl.semaphore_signal(barrier, inc=1, device_id=peer(d)[1], device_id_type=MESH)
    pl.semaphore_wait(barrier, count - 1)
    copies = []
    for d in range(1, count):
        index, where = peer(d)
        small = pltpu.make_async_remote_copy(
            src_ref=total_ref,
            dst_ref=held_total.at[d - 1],
            send_sem=send_total_sem.at[d - 1],
            recv_sem=recv_total_sem.at[d - 1],
            device_id=where,
            device_id_type=MESH,
        )
        small.start()
        large = pltpu.make_async_remote_copy(
            src_ref=send_ref.at[index],
            dst_ref=held.at[d - 1],
            send_sem=send_sem.at[d - 1],
            recv_sem=recv_sem.at[d - 1],
            device_id=where,
            device_id_type=MESH,
        )
        large.start()
        copies.append((small, large))
    for small, large in copies:
        small.wait()
        large.wait()
    total = total_ref[...]
    for d in range(1, count):
        total = total + held_total[d - 1]
    mean = jnp.sum(total, 1, keepdims=True) * (1.0 / pixels_all)
    for b in range(bands):
        flux = send_ref[me, 0, b].astype(jnp.float32)
        weight = send_ref[me, 1, b].astype(jnp.float32)
        for d in range(1, count):
            flux = flux + held[d - 1, 0, b].astype(jnp.float32)
            weight = weight + held[d - 1, 1, b].astype(jnp.float32)
        prior = prior_ref[b]
        columns = pl.ds(pl.multiple_of(epoch * part, LANES), part)
        template = template_ref[b, :, columns].astype(jnp.float32)
        depth = weight + prior
        coadd_ref[b] = ((flux + prior * template) / depth).astype(jnp.bfloat16)
        depth_ref[b] = (depth / mean[b : b + 1]).astype(jnp.bfloat16)


def on_device(
    slot_pixels, slot_tile, slot_offset, slot_frac, slot_sigma, clip_mask, slot_count, template, prior_weight
):
    sky = lax.axis_size("sky")
    epochs = lax.axis_size("epoch")
    count = sky * epochs
    slots, bands, rows, cols = slot_pixels.shape
    canvas = rows + 2 * MARGIN
    part = cols // epochs
    vmem = pl.BlockSpec(memory_space=pltpu.VMEM)
    smem = pl.BlockSpec(memory_space=pltpu.SMEM)
    templates = pl.pallas_call(
        functools.partial(gather_kernel, sky),
        out_shape=jax.ShapeDtypeStruct((sky,) + template.shape, jnp.bfloat16),
        in_specs=[vmem],
        out_specs=vmem,
        scratch_shapes=[
            pltpu.VMEM((sky - 1,) + template.shape, jnp.bfloat16),
            pltpu.SemaphoreType.DMA((sky - 1,)),
            pltpu.SemaphoreType.DMA((sky - 1,)),
        ],
        compiler_params=pltpu.CompilerParams(collective_id=0, has_side_effects=True),
        name="gather_templates",
    )(template)
    is_live = (jnp.arange(slots, dtype=jnp.int32) < slot_count[0]).astype(jnp.int32)
    mask_rows = clip_mask.shape[1]
    mask = (clip_mask * is_live[:, None, None]).astype(jnp.bfloat16)
    mask = jnp.pad(mask, ((0, 0), (0, -mask_rows % 8), (0, 0)))
    mask_rows = mask.shape[1]
    mask = mask.reshape(slots * mask_rows, mask.shape[2])
    taps = tap_weights(slot_frac).reshape(slots, 4 * REACH)
    sigma = slot_sigma.astype(jnp.float32)
    scale = CLIP_WIDTH * sigma
    sigmas = jnp.concatenate([scale, 1.0 / scale, 1.0 / (sigma * sigma)], 1)
    prior = prior_weight[:, :, None]
    patch = sky * rows + 2 * MARGIN
    sums = pltpu.VMEM((bands, patch, cols), jnp.float32)
    send, total = pl.pallas_call(
        functools.partial(warp_kernel, bands, sky, epochs, rows),
        out_shape=(
            jax.ShapeDtypeStruct((count, 2, bands, rows, part), jnp.bfloat16),
            jax.ShapeDtypeStruct((8 * -(-bands // 8), LANES), jnp.float32),
        ),
        in_specs=[smem] * 4 + [vmem] * 4,
        out_specs=(vmem, vmem),
        scratch_shapes=[
            sums,
            sums,
            sums,
            pltpu.VMEM((bands * rows + 8, cols + LANES), jnp.float32),
            pltpu.VMEM((slots, mask_rows, cols), jnp.float32),
        ],
        name="warp_slots",
    )(
        slot_tile[:, 0], slot_offset, taps, sigmas,
        slot_pixels.reshape(slots, bands * rows, cols), mask, templates, prior,
    )
    block = jax.ShapeDtypeStruct((bands, rows, part), jnp.bfloat16)
    return pl.pallas_call(
        functools.partial(exchange_kernel, bands, sky, epochs, sky * rows * cols),
        out_shape=(block, block),
        in_specs=[vmem] * 4,
        out_specs=(vmem, vmem),
        scratch_shapes=[
            pltpu.VMEM((count - 1,) + send.shape[1:], jnp.bfloat16),
            pltpu.VMEM((count - 1,) + total.shape, jnp.float32),
            pltpu.SemaphoreType.DMA((count - 1,)),
            pltpu.SemaphoreType.DMA((count - 1,)),
            pltpu.SemaphoreType.DMA((count - 1,)),
            pltpu.SemaphoreType.DMA((count - 1,)),
        ],
        compiler_params=pltpu.CompilerParams(collective_id=1, has_side_effects=True),
        name="exchange_sums",
    )(send, total, template, prior)


def solution(mesh):
    in_specs = (
        P(("groups", "sky", "epoch"), "band", None, None),
        P(("groups", "sky", "epoch"), None),
        P(("groups", "sky", "epoch"), None),
        P(("groups", "sky", "epoch"), None),
        P(("groups", "sky", "epoch"), "band"),
        P(("groups", "sky", "epoch"), None, None),
        P(("groups", "sky", "epoch")),
        P("band", ("groups", "sky"), None),
        P("band", ("groups", "sky")),
    )
    out_specs = (P("band", ("groups", "sky"), "epoch"), P("band", ("groups", "sky"), "epoch"))
    return jax.shard_map(
        on_device, mesh=mesh, in_specs=in_specs, out_specs=out_specs, check_vma=False
    )
```

time: 152 us -> 52.3 us (0.34)
  the two profiles are of different devices: /device:TPU:0 before, /device:TPU:14 now
where the time goes in v1:
time: 52.3 us; the launch traced here: 52 us
  Pallas kernels  43.5 us (83%)
  local copies, waits for them, and re-layouts  6.26 us (12%)
  between operations  1.33 us (3%)
  other arithmetic  0.89 us (2%)
    pallas_call x1, Pallas kernels, on_device(): pl.pallas_call(functools.partial(exchange_kernel, bands, sky, epochs, sky...  23.3 us
    pallas_call x1, Pallas kernels, on_device(): pl.pallas_call(functools.partial(gather_kernel, sky), out_shape=jax.Shape...  13.6 us
    pallas_call x1, Pallas kernels, on_device(): pl.pallas_call(functools.partial(warp_kernel, bands, sky, epochs, rows),...  6.64 us
    unnamed x16, local copies, waits for them, and re-layouts  4.15 us

profile of v1, /device:TPU:14, one launch (start us, length us, event | category | flops | bytes accessed | tf_op | source)
XLA Modules:
  0.0 52.0 jit_solution(11607049813541541551)
XLA Ops:
  1.3 0.0 copy-start.3
  1.3 0.7 %copy-done.3 = bf16[6,3]{0,1:T(4,128)(2,1)S(1)} copy-done((bf16[6,3]{0,1:T(4,128)(2,1)S(1)}, bf16[6,3]{0,1:T(4,128)(2,1)}, u32[]{:S(2)}) %copy-start.3) | copy-done | bytes 60
  2.0 0.0 copy-start.4
  2.0 0.1 copy.12
  2.1 0.6 %copy-done.4 = s32[6,2]{0,1:T(2,128)S(1)} copy-done((s32[6,2]{0,1:T(2,128)S(1)}, s32[6,2]{0,1:T(2,128)}, u32[]{:S(2)}) %copy-start.4) | copy-done | bytes 72
  2.6 0.0 copy-start.5
  2.7 0.7 %copy.13.offset_ref = s32[6,2]{1,0:T(8,128)} copy(s32[6,2]{0,1:T(2,128)S(1)} %copy-done.4) | data formatting | bytes 96 | tf_op args[2]
  3.3 0.0 copy-done.5
  3.3 0.1 copy.11
  3.4 0.0 copy-start.1
  3.4 0.1 fusion.16
  3.6 0.7 %reshape.32.taps_ref = f32[6,12]{1,0:T(8,128)} reshape(bf16[6,2,6]{2,1,0:T(2,128)(2,1)S(1)} %fusion.16) | data formatting | bytes 432 | tf_op jit(solution)/shard_map/reshape | solution.py:235
  4.2 0.7 %pad_maximum_fusion.sigma_ref = f32[6,9]{1,0:T(8,128)} fusion(f32[6,3]{1,0:T(8,128)S(1)} %get-tuple-element.9, f32[6,3]{1,0:T(8,128)S(1)} %get-tuple-element.8, f32[6,3]{1,0:T(8,128)S(1)} %get-tuple-element.7), kind=kLoop, calls=%fused_computation.42 | loop fusion | flops 108 | bytes 432 | tf_op jit(solution)/shard_map/concatenate | solution.py:238
  4.9 0.0 copy-done.1
  4.9 0.1 multiply_convert_fusion
  5.0 0.0 copy-start.2
  5.0 0.6 %pad_bitcast_fusion.mask_ref = bf16[48,16]{1,0:T(8,128)(2,1)} fusion(bf16[6,6,16]{2,1,0:T(8,128)(2,1)S(1)} %multiply_convert_fusion), kind=kLoop, calls=%fused_computation.7 | loop fusion | bytes 2688 | tf_op jit(solution)/shard_map/reshape | solution.py:234
  5.6 0.1 copy-done.2
  5.7 0.7 %copy.14.prior_ref = f32[3,32,1]{2,1,0:T(8,128)} copy(f32[3,32,1]{1,0,2:T(4,128)S(1)} %bitcast.8) | data formatting | bytes 768 | tf_op jit(solution)/shard_map/broadcast_in_dim | solution.py:239
  6.4 13.6 %gather_templates.1.template_ref = bf16[4,3,32,512]{3,2,1,0:T(8,128)(2,1)} custom-call(bf16[3,32,512]{2,1,0:T(8,128)(2,1)} %template_ref.1), custom_call_target="tpu_custom_call" | custom-call | tf_op jit(solution)/shard_map/gather_templates/pallas_call | solution.py:216
  20.0 6.6 %warp_slots.1 = (bf16[8,2,3,32,256]{4,3,2,1,0:T(8,128)(2,1)}, f32[8,128]{1,0:T(8,128)}) custom-call(s32[6]{0:T(128)} %bitcast.9, s32[6,2]{1,0:T(8,128)} %copy.13.offset_ref, f32[6,12]{1,0:T(8,128)} %reshape.32.taps_ref, f32[6,9]{1,0:T(8,128)} %pad_maximum_fusion.sigma_ref, bf16[6,96,512]{2,1,0:T(8,128)(2,1)} %bitcast.7, ...), custom_call_target="tpu_custom_call" | custom-call | tf_op jit(solution)/shard_map/warp_slots/pallas_call | solution.py:242
  26.6 23.3 %exchange_sums.1 = (bf16[3,32,256]{2,1,0:T(8,128)(2,1)}, bf16[3,32,256]{2,1,0:T(8,128)(2,1)}) custom-call(bf16[8,2,3,32,256]{4,3,2,1,0:T(8,128)(2,1)} %get-tuple-element.5.send_ref, f32[8,128]{1,0:T(8,128)} %get-tuple-element.6.total_ref, bf16[3,32,512]{2,1,0:T(8,128)(2,1)} %template_ref.1, f32[3,32,1]{2,1,0:T(8,128)} %copy.14.prior_ref), custom_call_target="tpu_custom_call" | custom-call | tf_op jit(solution)/shard_map/exchange_sums/pallas_call | solution.py:263
  49.9 0.0 copy-start
  49.9 1.4 %copy.19 = bf16[3,32,256]{2,1,0:T(8,128)(2,1)} copy(bf16[3,32,256]{2,1,0:T(8,128)(2,1)} %get-tuple-element.12) | data formatting | bytes 98304
  51.4 0.0 copy-done
  51.4 0.6 %copy.20 = bf16[3,32,256]{2,1,0:T(8,128)(2,1)} copy(bf16[3,32,256]{2,1,0:T(8,128)(2,1)S(1)} %copy-done) | data formatting | bytes 98304
  (3 shorter events, 0.0 us)
Async XLA Ops:
  1.3 0.7 %copy-start.3 = (bf16[6,3]{0,1:T(4,128)(2,1)S(1)}, bf16[6,3]{0,1:T(4,128)(2,1)}, u32[]{:S(2)}) copy-start(bf16[6,3]{0,1:T(4,128)(2,1)} %param.14) | copy-start | bytes 112
  2.0 0.7 %copy-start.4 = (s32[6,2]{0,1:T(2,128)S(1)}, s32[6,2]{0,1:T(2,128)}, u32[]{:S(2)}) copy-start(s32[6,2]{0,1:T(2,128)} %param.12) | copy-start | bytes 148
  2.6 0.7 %copy-start.5 = (bf16[6,2]{0,1:T(2,128)(2,1)S(1)}, bf16[6,2]{0,1:T(2,128)(2,1)}, u32[]{:S(2)}) copy-start(bf16[6,2]{0,1:T(2,128)(2,1)} %param.13) | copy-start | bytes 76
  3.4 1.5 %copy-start.1 = (s32[6,6,16]{2,1,0:T(8,128)S(1)}, s32[6,6,16]{2,1,0:T(8,128)}, u32[]{:S(2)}) copy-start(s32[6,6,16]{2,1,0:T(8,128)} %param.15) | copy-start | bytes 6916
  5.0 0.7 %copy-start.2 = (f32[3,32]{1,0:T(4,128)S(1)}, f32[3,32]{1,0:T(4,128)}, u32[]{:S(2)}) copy-start(f32[3,32]{1,0:T(4,128)} %param.18) | copy-start | bytes 1156
  49.9 1.4 %copy-start = (bf16[3,32,256]{2,1,0:T(8,128)(2,1)S(1)}, bf16[3,32,256]{2,1,0:T(8,128)(2,1)}, u32[]{:S(2)}) copy-start(bf16[3,32,256]{2,1,0:T(8,128)(2,1)} %get-tuple-element.13) | copy-start | bytes 147460

commit v2 on v1

--- a/solution.py
+++ b/solution.py
@@ -12,6 +12,7 @@
 REACH = 3
 LANES = 128
 CLIP_WIDTH = 3.0
+CELL_TYPE = jnp.bfloat16
 MESH = pl.DeviceIdType.MESH
 
 
@@ -57,8 +58,8 @@
     bands, sky, epochs, rows,
     tile_ref, offset_ref, taps_ref, sigma_ref,
     pixels_ref, mask_ref, template_ref, prior_ref,
-    send_ref, total_ref,
-    framed, flux, weights, source, wide_mask,
+    send_ref, total_ref, rows_ref, cells_ref,
+    framed, flux, cells, source, wide_mask,
 ):
     slots = pixels_ref.shape[0]
     cols = pixels_ref.shape[2]
@@ -69,7 +70,14 @@
     mask_cols = mask_ref.shape[1]
 
     flux[...] = jnp.zeros_like(flux)
-    weights[...] = jnp.zeros_like(weights)
+    cells[...] = jnp.zeros_like(cells)
+    total_ref[...] = jnp.zeros_like(total_ref)
+    rows_ref[...] = jnp.zeros_like(rows_ref)
+    lane = lax.broadcasted_iota(jnp.int32, (sky, rows_ref.shape[2]), 1)
+    patch_row = lax.broadcasted_iota(jnp.int32, lane.shape, 0) * rows + lax.rem(lane, rows)
+    canvas_row = lax.broadcasted_iota(jnp.int32, (canvas, 1), 0) - MARGIN
+    group = rows // BLOCK_ROWS
+    first = MARGIN // BLOCK_ROWS
     edge = jnp.zeros((bands, MARGIN, cols), jnp.float32)
     framed[:, :MARGIN] = edge
     framed[:, MARGIN + sky * rows :] = edge
@@ -105,12 +113,33 @@
             row_table = row_table + jnp.where(gap == dy + REACH - tap, taps_ref[p, tap], 0.0)
         row_cover = jnp.clip(jnp.sum(row_table, 1, keepdims=True), 0.0, 1.0)
         row_table = row_table.astype(jnp.bfloat16)
+        start = pl.multiple_of(tile_ref[p] * rows, 8)
+        global_row = canvas_row + start
+        row_cover = jnp.where((global_row >= 0) & (global_row < sky * rows), row_cover, 0.0)
         pieces = []
         for i in range(blocks):
             cover = row_cover[i * BLOCK_ROWS : (i + 1) * BLOCK_ROWS]
-            pieces.append(wide_mask[p, i : i + 1] * cover * col_cover)
+            cell_row = wide_mask[p, i : i + 1] * col_cover[:1]
+            cells[tile_ref[p] * group + i, pl.ds(p, 1)] = cell_row
+            pieces.append(cell_row * cover)
         plane = jnp.concatenate(pieces, 0)
-        start = pl.multiple_of(tile_ref[p] * rows, 8)
+        tile_row = patch_row - start - dy
+        profile = jnp.zeros(lane.shape, jnp.float32)
+        for tap in range(2 * REACH):
+            from_row = tile_row + (tap - REACH)
+            profile = profile + jnp.where((from_row >= 0) & (from_row < rows), taps_ref[p, tap], 0.0)
+        profile = jnp.clip(profile, 0.0, 1.0)
+        inverse = jnp.zeros(lane.shape, jnp.float32)
+        along = jnp.sum(plane, 0, keepdims=True)
+        folded = along[:, :LANES]
+        for c in range(1, cols // LANES):
+            folded = folded + along[:, c * LANES : (c + 1) * LANES]
+        for b in range(bands):
+            inverse = jnp.where(lane // rows == b, sigma_ref[p, 2 * bands + b], inverse)
+            total_ref[b : b + 1] += folded * sigma_ref[p, 2 * bands + b]
+        profile = profile * inverse
+        for s in range(sky):
+            rows_ref[s, pl.ds(p, 1)] = profile[s : s + 1]
         for b in range(bands):
             warped = jnp.dot(
                 row_table, columns[b * rows : (b + 1) * rows], preferred_element_type=jnp.float32
@@ -120,7 +149,6 @@
             clipped = frame + scale * jnp.tanh((warped - frame) * sigma_ref[p, bands + b])
             weight = plane * sigma_ref[p, 2 * bands + b]
             flux[b, pl.ds(start, canvas)] += weight * clipped
-            weights[b, pl.ds(start, canvas)] += weight
         return carry
 
     lax.fori_loop(0, slots, one_slot, 0)
@@ -128,23 +156,19 @@
         near = slice(MARGIN + s * rows, MARGIN + (s + 1) * rows)
         for e in range(epochs):
             far = slice(e * part, (e + 1) * part)
-            send_ref[s * epochs + e, 0] = flux[:, near, far].astype(jnp.bfloat16)
-            send_ref[s * epochs + e, 1] = weights[:, near, far].astype(jnp.bfloat16)
-    total_ref[...] = jnp.zeros_like(total_ref)
+            send_ref[s * epochs + e] = flux[:, near, far].astype(jnp.bfloat16)
+            for g in range(group):
+                cells_ref[s * epochs + e, g] = cells[first + s * group + g, :, far].astype(CELL_TYPE)
     for b in range(bands):
-        along = jnp.sum(weights[b, MARGIN : MARGIN + sky * rows], 0, keepdims=True)
-        folded = along[:, :LANES]
-        for c in range(1, cols // LANES):
-            folded = folded + along[:, c * LANES : (c + 1) * LANES]
         prior = jnp.sum(prior_ref[b], 0, keepdims=True)
-        total_ref[b : b + 1] = folded + prior * (part / LANES)
+        total_ref[b : b + 1] += prior * (part / LANES)
 
 
 def exchange_kernel(
     bands, sky, epochs, pixels_all,
-    send_ref, total_ref, template_ref, prior_ref,
+    send_ref, total_ref, rows_ref, cells_ref, template_ref, prior_ref,
     coadd_ref, depth_ref,
-    held, held_total, send_sem, recv_sem, send_total_sem, recv_total_sem,
+    held, held_total, held_rows, held_cells, send_sem, recv_sem,
 ):
     count = sky * epochs
     part = coadd_ref.shape[2]
@@ -162,38 +186,53 @@
     copies = []
     for d in range(1, count):
         index, where = peer(d)
-        small = pltpu.make_async_remote_copy(
-            src_ref=total_ref,
-            dst_ref=held_total.at[d - 1],
-            send_sem=send_total_sem.at[d - 1],
-            recv_sem=recv_total_sem.at[d - 1],
-            device_id=where,
-            device_id_type=MESH,
+        sky_index = index // epochs
+        moves = (
+            (total_ref, held_total),
+            (rows_ref.at[sky_index], held_rows),
+            (cells_ref.at[index], held_cells),
+            (send_ref.at[index], held),
         )
-        small.start()
-        large = pltpu.make_async_remote_copy(
-            src_ref=send_ref.at[index],
-            dst_ref=held.at[d - 1],
-            send_sem=send_sem.at[d - 1],
-            recv_sem=recv_sem.at[d - 1],
-            device_id=where,
-            device_id_type=MESH,
-        )
-        large.start()
-        copies.append((small, large))
-    for small, large in copies:
-        small.wait()
-        large.wait()
+        for k, (src, dst) in enumerate(moves):
+            copy = pltpu.make_async_remote_copy(
+                src_ref=src,
+                dst_ref=dst.at[d - 1],
+                send_sem=send_sem.at[k, d - 1],
+                recv_sem=recv_sem.at[k, d - 1],
+                device_id=where,
+                device_id_type=MESH,
+            )
+            copy.start()
+            copies.append(copy)
+    for copy in copies:
+        copy.wait()
     total = total_ref[...]
     for d in range(1, count):
         total = total + held_total[d - 1]
     mean = jnp.sum(total, 1, keepdims=True) * (1.0 / pixels_all)
+    rows = template_ref.shape[1]
+    group = rows // BLOCK_ROWS
+    sky_me = lax.axis_index("sky")
+
+    def weight_from(profile, cell):
+        block = lax.broadcasted_iota(jnp.int32, profile.shape, 1) // BLOCK_ROWS
+        block = lax.rem(block, group)
+        wide = [jnp.where(block == g, profile, 0.0) for g in range(group)]
+        wide = jnp.concatenate(wide, 0).astype(jnp.bfloat16)
+        cell = jnp.concatenate([cell[g].astype(jnp.float32) for g in range(group)], 0)
+        return lax.dot_general(
+            wide, cell.astype(jnp.bfloat16), (((0,), (0,)), ((), ())),
+            preferred_element_type=jnp.float32,
+        )
+
+    weights = weight_from(rows_ref[sky_me], cells_ref[me])
+    for d in range(1, count):
+        weights = weights + weight_from(held_rows[d - 1], held_cells[d - 1])
     for b in range(bands):
-        flux = send_ref[me, 0, b].astype(jnp.float32)
-        weight = send_ref[me, 1, b].astype(jnp.float32)
+        flux = send_ref[me, b].astype(jnp.float32)
+        weight = weights[b * rows : (b + 1) * rows]
         for d in range(1, count):
-            flux = flux + held[d - 1, 0, b].astype(jnp.float32)
-            weight = weight + held[d - 1, 1, b].astype(jnp.float32)
+            flux = flux + held[d - 1, b].astype(jnp.float32)
         prior = prior_ref[b]
         columns = pl.ds(pl.multiple_of(epoch * part, LANES), part)
         template = template_ref[b, :, columns].astype(jnp.float32)
@@ -239,18 +278,24 @@
     prior = prior_weight[:, :, None]
     patch = sky * rows + 2 * MARGIN
     sums = pltpu.VMEM((bands, patch, cols), jnp.float32)
-    send, total = pl.pallas_call(
+    held_slots = slots + -slots % 8
+    lanes = bands * rows + -(bands * rows) % LANES
+    group = rows // BLOCK_ROWS
+    patch_blocks = sky * group + 2 * MARGIN // BLOCK_ROWS
+    send, total, row_factor, cell_factor = pl.pallas_call(
         functools.partial(warp_kernel, bands, sky, epochs, rows),
         out_shape=(
-            jax.ShapeDtypeStruct((count, 2, bands, rows, part), jnp.bfloat16),
+            jax.ShapeDtypeStruct((count, bands, rows, part), jnp.bfloat16),
             jax.ShapeDtypeStruct((8 * -(-bands // 8), LANES), jnp.float32),
+            jax.ShapeDtypeStruct((sky, held_slots, lanes), jnp.float32),
+            jax.ShapeDtypeStruct((count, group, held_slots, part), CELL_TYPE),
         ),
         in_specs=[smem] * 4 + [vmem] * 4,
-        out_specs=(vmem, vmem),
+        out_specs=(vmem,) * 4,
         scratch_shapes=[
             sums,
             sums,
-            sums,
+            pltpu.VMEM((patch_blocks, held_slots, cols), jnp.float32),
             pltpu.VMEM((bands * rows + 8, cols + LANES), jnp.float32),
             pltpu.VMEM((slots, mask_rows, cols), jnp.float32),
         ],
@@ -263,19 +308,19 @@
     return pl.pallas_call(
         functools.partial(exchange_kernel, bands, sky, epochs, sky * rows * cols),
         out_shape=(block, block),
-        in_specs=[vmem] * 4,
+        in_specs=[vmem] * 6,
         out_specs=(vmem, vmem),
         scratch_shapes=[
             pltpu.VMEM((count - 1,) + send.shape[1:], jnp.bfloat16),
             pltpu.VMEM((count - 1,) + total.shape, jnp.float32),
-            pltpu.SemaphoreType.DMA((count - 1,)),
-            pltpu.SemaphoreType.DMA((count - 1,)),
-            pltpu.SemaphoreType.DMA((count - 1,)),
-            pltpu.SemaphoreType.DMA((count - 1,)),
+            pltpu.VMEM((count - 1,) + row_factor.shape[1:], jnp.float32),
+            pltpu.VMEM((count - 1,) + cell_factor.shape[1:], CELL_TYPE),
+            pltpu.SemaphoreType.DMA((4, count - 1)),
+            pltpu.SemaphoreType.DMA((4, count - 1)),
         ],
         compiler_params=pltpu.CompilerParams(collective_id=1, has_side_effects=True),
         name="exchange_sums",
-    )(send, total, template, prior)
+    )(send, total, row_factor, cell_factor, template, prior)
 
 
 def solution(mesh):

time: 52.3 us -> 47.7 us (0.912)
  Pallas kernels: 43.5 us -> 38.8 us
    pallas_call x1, Pallas kernels: 23.3 us -> 18.8 us  [on_device(): pl.pallas_call(functools.partial(exchange_kernel, bands, sky, epochs, sky...]
where the time goes in v2:
time: 47.7 us; the launch traced here: 47.3 us
  Pallas kernels  38.8 us (81%)
  local copies, waits for them, and re-layouts  6.26 us (13%)
  between operations  1.33 us (3%)
  other arithmetic  0.9 us (2%)
    pallas_call x1, Pallas kernels, on_device(): pl.pallas_call(functools.partial(exchange_kernel, bands, sky, epochs, sky...  18.8 us
    pallas_call x1, Pallas kernels, on_device(): pl.pallas_call(functools.partial(gather_kernel, sky), out_shape=jax.Shape...  13.6 us
    pallas_call x1, Pallas kernels, on_device(): pl.pallas_call(functools.partial(warp_kernel, bands, sky, epochs, rows),...  6.48 us
    unnamed x16, local copies, waits for them, and re-layouts  4.16 us

profile of v2, /device:TPU:14, one launch (start us, length us, event | category | flops | bytes accessed | tf_op | source)
XLA Modules:
  0.0 47.3 jit_solution(2415537651620100958)
XLA Ops:
  1.3 0.0 copy-start.3
  1.3 0.7 %copy-done.3 = bf16[6,3]{0,1:T(4,128)(2,1)S(1)} copy-done((bf16[6,3]{0,1:T(4,128)(2,1)S(1)}, bf16[6,3]{0,1:T(4,128)(2,1)}, u32[]{:S(2)}) %copy-start.3) | copy-done | bytes 60
  2.0 0.0 copy-start.4
  2.0 0.1 copy.12
  2.1 0.6 %copy-done.4 = s32[6,2]{0,1:T(2,128)S(1)} copy-done((s32[6,2]{0,1:T(2,128)S(1)}, s32[6,2]{0,1:T(2,128)}, u32[]{:S(2)}) %copy-start.4) | copy-done | bytes 72
  2.6 0.0 copy-start.5
  2.7 0.7 %copy.13.offset_ref = s32[6,2]{1,0:T(8,128)} copy(s32[6,2]{0,1:T(2,128)S(1)} %copy-done.4) | data formatting | bytes 96 | tf_op args[2]
  3.3 0.0 copy-done.5
  3.3 0.1 copy.11
  3.4 0.0 copy-start.1
  3.4 0.1 fusion.16
  3.6 0.7 %reshape.32.taps_ref = f32[6,12]{1,0:T(8,128)} reshape(bf16[6,2,6]{2,1,0:T(2,128)(2,1)S(1)} %fusion.16) | data formatting | bytes 432 | tf_op jit(solution)/shard_map/reshape | solution.py:274
  4.3 0.7 %pad_maximum_fusion.sigma_ref = f32[6,9]{1,0:T(8,128)} fusion(f32[6,3]{1,0:T(8,128)S(1)} %get-tuple-element.13, f32[6,3]{1,0:T(8,128)S(1)} %get-tuple-element.12, f32[6,3]{1,0:T(8,128)S(1)} %get-tuple-element.11), kind=kLoop, calls=%fused_computation.42 | loop fusion | flops 108 | bytes 432 | tf_op jit(solution)/shard_map/concatenate | solution.py:277
  4.9 0.0 copy-done.1
  4.9 0.1 multiply_convert_fusion
  5.0 0.0 copy-start.2
  5.0 0.6 %pad_bitcast_fusion.mask_ref = bf16[48,16]{1,0:T(8,128)(2,1)} fusion(bf16[6,6,16]{2,1,0:T(8,128)(2,1)S(1)} %multiply_convert_fusion), kind=kLoop, calls=%fused_computation.7 | loop fusion | bytes 2688 | tf_op jit(solution)/shard_map/reshape | solution.py:273
  5.6 0.1 copy-done.2
  5.7 0.7 %copy.14.prior_ref = f32[3,32,1]{2,1,0:T(8,128)} copy(f32[3,32,1]{1,0,2:T(4,128)S(1)} %bitcast.8) | data formatting | bytes 768 | tf_op jit(solution)/shard_map/broadcast_in_dim | solution.py:278
  6.4 13.6 %gather_templates.1.template_ref = bf16[4,3,32,512]{3,2,1,0:T(8,128)(2,1)} custom-call(bf16[3,32,512]{2,1,0:T(8,128)(2,1)} %template_ref.1), custom_call_target="tpu_custom_call" | custom-call | tf_op jit(solution)/shard_map/gather_templates/pallas_call | solution.py:255
  20.0 6.5 %warp_slots.1 = (bf16[8,3,32,256]{3,2,1,0:T(8,128)(2,1)}, f32[8,128]{1,0:T(8,128)}, f32[4,8,128]{2,1,0:T(8,128)}, bf16[8,4,8,256]{3,2,1,0:T(8,128)(2,1)}) custom-call(s32[6]{0:T(128)} %bitcast.9, s32[6,2]{1,0:T(8,128)} %copy.13.offset_ref, f32[6,12]{1,0:T(8,128)} %reshape.32.taps_ref, f32[6,9]{1,0:T(8,128)} %pad_maximum_fusion.sigma_ref, ...), custom_call_target="tpu_custom_call" | custom-call | tf_op jit(solution)/shard_map/warp_slots/pallas_call | solution.py:285
  26.5 18.8 %exchange_sums.1 = (bf16[3,32,256]{2,1,0:T(8,128)(2,1)}, bf16[3,32,256]{2,1,0:T(8,128)(2,1)}) custom-call(bf16[8,3,32,256]{3,2,1,0:T(8,128)(2,1)} %get-tuple-element.7.send_ref, f32[8,128]{1,0:T(8,128)} %get-tuple-element.8.total_ref, f32[4,8,128]{2,1,0:T(8,128)} %get-tuple-element.9.rows_ref, bf16[8,4,8,256]{3,2,1,0:T(8,128)(2,1)} %get-tuple-element.10.cells_ref, ...), custom_call_target="tpu_custom_call" | custom-call | tf_op jit(solution)/shard_map/exchange_sums/pallas_call | solution.py:308
  45.3 0.0 copy-start
  45.3 1.4 %copy.19 = bf16[3,32,256]{2,1,0:T(8,128)(2,1)} copy(bf16[3,32,256]{2,1,0:T(8,128)(2,1)} %get-tuple-element.16) | data formatting | bytes 98304
  46.7 0.0 copy-done
  46.7 0.6 %copy.20 = bf16[3,32,256]{2,1,0:T(8,128)(2,1)} copy(bf16[3,32,256]{2,1,0:T(8,128)(2,1)S(1)} %copy-done) | data formatting | bytes 98304
  (3 shorter events, 0.0 us)
Async XLA Ops:
  1.3 0.7 %copy-start.3 = (bf16[6,3]{0,1:T(4,128)(2,1)S(1)}, bf16[6,3]{0,1:T(4,128)(2,1)}, u32[]{:S(2)}) copy-start(bf16[6,3]{0,1:T(4,128)(2,1)} %param.14) | copy-start | bytes 112
  2.0 0.7 %copy-start.4 = (s32[6,2]{0,1:T(2,128)S(1)}, s32[6,2]{0,1:T(2,128)}, u32[]{:S(2)}) copy-start(s32[6,2]{0,1:T(2,128)} %param.12) | copy-start | bytes 148
  2.6 0.7 %copy-start.5 = (bf16[6,2]{0,1:T(2,128)(2,1)S(1)}, bf16[6,2]{0,1:T(2,128)(2,1)}, u32[]{:S(2)}) copy-start(bf16[6,2]{0,1:T(2,128)(2,1)} %param.13) | copy-start | bytes 76
  3.4 1.5 %copy-start.1 = (s32[6,6,16]{2,1,0:T(8,128)S(1)}, s32[6,6,16]{2,1,0:T(8,128)}, u32[]{:S(2)}) copy-start(s32[6,6,16]{2,1,0:T(8,128)} %param.15) | copy-start | bytes 6916
  5.0 0.7 %copy-start.2 = (f32[3,32]{1,0:T(4,128)S(1)}, f32[3,32]{1,0:T(4,128)}, u32[]{:S(2)}) copy-start(f32[3,32]{1,0:T(4,128)} %param.18) | copy-start | bytes 1156
  45.3 1.4 %copy-start = (bf16[3,32,256]{2,1,0:T(8,128)(2,1)S(1)}, bf16[3,32,256]{2,1,0:T(8,128)(2,1)}, u32[]{:S(2)}) copy-start(bf16[3,32,256]{2,1,0:T(8,128)(2,1)} %get-tuple-element.17) | copy-start | bytes 147460

commit v3 on v2

--- a/solution.py
+++ b/solution.py
@@ -23,7 +23,7 @@
 
 def tap_weights(fractions):
     steps_back = jnp.arange(-REACH, REACH, dtype=jnp.int32)
-    distance = (-steps_back).astype(jnp.float32) - fractions.astype(jnp.float32)[..., None]
+    distance = (-steps_back).astype(jnp.float32)[:, None] - fractions.astype(jnp.float32)[:, None]
     rounded = lanczos(distance).astype(jnp.bfloat16)
     return lax.optimization_barrier(rounded).astype(jnp.float32)
 
@@ -56,10 +56,10 @@
 
 def warp_kernel(
     bands, sky, epochs, rows,
-    tile_ref, offset_ref, taps_ref, sigma_ref,
+    tile_ref, offset_ref, count_ref, param_ref,
     pixels_ref, mask_ref, template_ref, prior_ref,
     send_ref, total_ref, rows_ref, cells_ref,
-    framed, flux, cells, source, wide_mask,
+    framed, flux, cells, source,
 ):
     slots = pixels_ref.shape[0]
     cols = pixels_ref.shape[2]
@@ -67,7 +67,7 @@
     canvas = rows + 2 * MARGIN
     blocks = canvas // BLOCK_ROWS
     part = cols // epochs
-    mask_cols = mask_ref.shape[1]
+    mask_cols = mask_ref.shape[2]
 
     flux[...] = jnp.zeros_like(flux)
     cells[...] = jnp.zeros_like(cells)
@@ -88,9 +88,6 @@
     cell = lax.broadcasted_iota(jnp.int32, (mask_cols, cols), 0)
     column = lax.broadcasted_iota(jnp.int32, (mask_cols, cols), 1) // (cols // mask_cols)
     spread = jnp.where(cell == column, 1.0, 0.0).astype(jnp.bfloat16)
-    wide_mask[...] = jnp.dot(
-        mask_ref[...], spread, preferred_element_type=jnp.float32
-    ).reshape(wide_mask.shape)
     gap = (
         lax.broadcasted_iota(jnp.int32, (canvas, rows), 0)
         - lax.broadcasted_iota(jnp.int32, (canvas, rows), 1)
@@ -98,28 +95,32 @@
     )
 
     def one_slot(p, carry):
-        dy, dx = offset_ref[p, 0], offset_ref[p, 1]
+        dy, dx = offset_ref[0, p], offset_ref[1, p]
         source[: bands * rows, :cols] = pixels_ref[p].astype(jnp.float32)
         base = pltpu.roll(source[...], lax.rem(dx + padded, padded), 1)
-        summed = taps_ref[p, 2 * REACH + REACH] * base
+        summed = param_ref[2 * REACH + REACH, p] * base
         for tap in range(2 * REACH):
             if tap != REACH:
                 moved = pltpu.roll(base, (REACH - tap) % padded, 1)
-                summed = summed + taps_ref[p, 2 * REACH + tap] * moved
+                summed = summed + param_ref[2 * REACH + tap, p] * moved
         columns = summed[: bands * rows, :cols].astype(jnp.bfloat16)
         col_cover = jnp.clip(summed[bands * rows :, :cols], 0.0, 1.0)
         row_table = jnp.zeros((canvas, rows), jnp.float32)
         for tap in range(2 * REACH):
-            row_table = row_table + jnp.where(gap == dy + REACH - tap, taps_ref[p, tap], 0.0)
+            row_table = row_table + jnp.where(gap == dy + REACH - tap, param_ref[tap, p], 0.0)
         row_cover = jnp.clip(jnp.sum(row_table, 1, keepdims=True), 0.0, 1.0)
         row_table = row_table.astype(jnp.bfloat16)
         start = pl.multiple_of(tile_ref[p] * rows, 8)
         global_row = canvas_row + start
         row_cover = jnp.where((global_row >= 0) & (global_row < sky * rows), row_cover, 0.0)
+        live = jnp.where(p < count_ref[0], 1.0, 0.0)
+        wide_mask = live * jnp.dot(
+            mask_ref[p].astype(jnp.bfloat16), spread, preferred_element_type=jnp.float32
+        )
         pieces = []
         for i in range(blocks):
             cover = row_cover[i * BLOCK_ROWS : (i + 1) * BLOCK_ROWS]
-            cell_row = wide_mask[p, i : i + 1] * col_cover[:1]
+            cell_row = wide_mask[i : i + 1] * col_cover[:1]
             cells[tile_ref[p] * group + i, pl.ds(p, 1)] = cell_row
             pieces.append(cell_row * cover)
         plane = jnp.concatenate(pieces, 0)
@@ -127,7 +128,7 @@
         profile = jnp.zeros(lane.shape, jnp.float32)
         for tap in range(2 * REACH):
             from_row = tile_row + (tap - REACH)
-            profile = profile + jnp.where((from_row >= 0) & (from_row < rows), taps_ref[p, tap], 0.0)
+            profile = profile + jnp.where((from_row >= 0) & (from_row < rows), param_ref[tap, p], 0.0)
         profile = jnp.clip(profile, 0.0, 1.0)
         inverse = jnp.zeros(lane.shape, jnp.float32)
         along = jnp.sum(plane, 0, keepdims=True)
@@ -135,8 +136,8 @@
         for c in range(1, cols // LANES):
             folded = folded + along[:, c * LANES : (c + 1) * LANES]
         for b in range(bands):
-            inverse = jnp.where(lane // rows == b, sigma_ref[p, 2 * bands + b], inverse)
-            total_ref[b : b + 1] += folded * sigma_ref[p, 2 * bands + b]
+            inverse = jnp.where(lane // rows == b, param_ref[4 * REACH + 2 * bands + b, p], inverse)
+            total_ref[b : b + 1] += folded * param_ref[4 * REACH + 2 * bands + b, p]
         profile = profile * inverse
         for s in range(sky):
             rows_ref[s, pl.ds(p, 1)] = profile[s : s + 1]
@@ -145,9 +146,9 @@
                 row_table, columns[b * rows : (b + 1) * rows], preferred_element_type=jnp.float32
             )
             frame = framed[b, pl.ds(start, canvas)]
-            scale = sigma_ref[p, b]
-            clipped = frame + scale * jnp.tanh((warped - frame) * sigma_ref[p, bands + b])
-            weight = plane * sigma_ref[p, 2 * bands + b]
+            scale = param_ref[4 * REACH + b, p]
+            clipped = frame + scale * jnp.tanh((warped - frame) * param_ref[4 * REACH + bands + b, p])
+            weight = plane * param_ref[4 * REACH + 2 * bands + b, p]
             flux[b, pl.ds(start, canvas)] += weight * clipped
         return carry
 
@@ -160,7 +161,7 @@
             for g in range(group):
                 cells_ref[s * epochs + e, g] = cells[first + s * group + g, :, far].astype(CELL_TYPE)
     for b in range(bands):
-        prior = jnp.sum(prior_ref[b], 0, keepdims=True)
+        prior = jnp.sum(prior_ref[b : b + 1], 1, keepdims=True)
         total_ref[b : b + 1] += prior * (part / LANES)
 
 
@@ -184,27 +185,28 @@
         pl.semaphore_signal(barrier, inc=1, device_id=peer(d)[1], device_id_type=MESH)
     pl.semaphore_wait(barrier, count - 1)
     copies = []
-    for d in range(1, count):
-        index, where = peer(d)
-        sky_index = index // epochs
-        moves = (
-            (total_ref, held_total),
-            (rows_ref.at[sky_index], held_rows),
-            (cells_ref.at[index], held_cells),
-            (send_ref.at[index], held),
-        )
-        for k, (src, dst) in enumerate(moves):
-            copy = pltpu.make_async_remote_copy(
-                src_ref=src,
-                dst_ref=dst.at[d - 1],
-                send_sem=send_sem.at[k, d - 1],
-                recv_sem=recv_sem.at[k, d - 1],
-                device_id=where,
-                device_id_type=MESH,
+    for large in (False, True):
+        for d in range(1, count):
+            index, where = peer(d)
+            moves = (
+                (send_ref.at[index], held),
+                (total_ref, held_total),
+                (rows_ref.at[index // epochs], held_rows),
+                (cells_ref.at[index], held_cells),
             )
-            copy.start()
-            copies.append(copy)
-    for copy in copies:
+            for k, (src, dst) in enumerate(moves):
+                if large == (k == 0):
+                    copy = pltpu.make_async_remote_copy(
+                        src_ref=src,
+                        dst_ref=dst.at[d - 1],
+                        send_sem=send_sem.at[k, d - 1],
+                        recv_sem=recv_sem.at[k, d - 1],
+                        device_id=where,
+                        device_id_type=MESH,
+                    )
+                    copy.start()
+                    copies.append(copy)
+    for copy in copies[: 1 - count]:
         copy.wait()
     total = total_ref[...]
     for d in range(1, count):
@@ -212,6 +214,9 @@
     mean = jnp.sum(total, 1, keepdims=True) * (1.0 / pixels_all)
     rows = template_ref.shape[1]
     group = rows // BLOCK_ROWS
+    diagonal = lax.broadcasted_iota(jnp.int32, (rows, rows), 0) == lax.broadcasted_iota(
+        jnp.int32, (rows, rows), 1
+    )
     sky_me = lax.axis_index("sky")
 
     def weight_from(profile, cell):
@@ -228,12 +233,14 @@
     weights = weight_from(rows_ref[sky_me], cells_ref[me])
     for d in range(1, count):
         weights = weights + weight_from(held_rows[d - 1], held_cells[d - 1])
+    for copy in copies[1 - count :]:
+        copy.wait()
     for b in range(bands):
         flux = send_ref[me, b].astype(jnp.float32)
         weight = weights[b * rows : (b + 1) * rows]
         for d in range(1, count):
             flux = flux + held[d - 1, b].astype(jnp.float32)
-        prior = prior_ref[b]
+        prior = jnp.sum(jnp.where(diagonal, prior_ref[b : b + 1], 0.0), 1, keepdims=True)
         columns = pl.ds(pl.multiple_of(epoch * part, LANES), part)
         template = template_ref[b, :, columns].astype(jnp.float32)
         depth = weight + prior
@@ -265,17 +272,10 @@
         compiler_params=pltpu.CompilerParams(collective_id=0, has_side_effects=True),
         name="gather_templates",
     )(template)
-    is_live = (jnp.arange(slots, dtype=jnp.int32) < slot_count[0]).astype(jnp.int32)
-    mask_rows = clip_mask.shape[1]
-    mask = (clip_mask * is_live[:, None, None]).astype(jnp.bfloat16)
-    mask = jnp.pad(mask, ((0, 0), (0, -mask_rows % 8), (0, 0)))
-    mask_rows = mask.shape[1]
-    mask = mask.reshape(slots * mask_rows, mask.shape[2])
-    taps = tap_weights(slot_frac).reshape(slots, 4 * REACH)
-    sigma = slot_sigma.astype(jnp.float32)
+    taps = tap_weights(slot_frac.T).reshape(4 * REACH, slots)
+    sigma = slot_sigma.T.astype(jnp.float32)
     scale = CLIP_WIDTH * sigma
-    sigmas = jnp.concatenate([scale, 1.0 / scale, 1.0 / (sigma * sigma)], 1)
-    prior = prior_weight[:, :, None]
+    params = jnp.concatenate([taps, scale, 1.0 / scale, 1.0 / (sigma * sigma)], 0)
     patch = sky * rows + 2 * MARGIN
     sums = pltpu.VMEM((bands, patch, cols), jnp.float32)
     held_slots = slots + -slots % 8
@@ -297,12 +297,11 @@
             sums,
             pltpu.VMEM((patch_blocks, held_slots, cols), jnp.float32),
             pltpu.VMEM((bands * rows + 8, cols + LANES), jnp.float32),
-            pltpu.VMEM((slots, mask_rows, cols), jnp.float32),
         ],
         name="warp_slots",
     )(
-        slot_tile[:, 0], slot_offset, taps, sigmas,
-        slot_pixels.reshape(slots, bands * rows, cols), mask, templates, prior,
+        slot_tile[:, 0], slot_offset.T, slot_count, params,
+        slot_pixels.reshape(slots, bands * rows, cols), clip_mask, templates, prior_weight,
     )
     block = jax.ShapeDtypeStruct((bands, rows, part), jnp.bfloat16)
     return pl.pallas_call(
@@ -320,7 +319,7 @@
         ],
         compiler_params=pltpu.CompilerParams(collective_id=1, has_side_effects=True),
         name="exchange_sums",
-    )(send, total, row_factor, cell_factor, template, prior)
+    )(send, total, row_factor, cell_factor, template, prior_weight)
 
 
 def solution(mesh):

time: 47.7 us -> 45 us (0.943)
  local copies, waits for them, and re-layouts: 6.26 us -> 4.35 us
  other arithmetic: 0.9 us -> 0.24 us
    reshape x2 -> x1, local copies, waits for them, and re-layouts: 1.28 us -> 0.08 us  [on_device(): taps = tap_weights(slot_frac.T).reshape(4 * REACH, slots)]
    broadcast_in_dim x1 -> x0, local copies, waits for them, and re-layouts: 0.72 us -> none  [on_device(): prior = prior_weight[:, :, None]]
    concatenate x0 -> x1, local copies, waits for them, and re-layouts: none -> 0.71 us  [on_device(): jnp.concatenate([taps, scale, 1.0 / scale, 1.0 / (sigma * sigma)], 0)]
    unnamed x16 -> x9, local copies, waits for them, and re-layouts: 4.16 us -> 3.48 us
    concatenate x1, other arithmetic: 0.68 us -> 0.08 us  [on_device(): jnp.concatenate([taps, scale, 1.0 / scale, 1.0 / (sigma * sigma)], 0)]
where the time goes in v3:
time: 45 us; the launch traced here: 44.3 us
  Pallas kernels  38.4 us (85%)
  local copies, waits for them, and re-layouts  4.35 us (10%)
  between operations  1.32 us (3%)
    pallas_call x1, Pallas kernels, on_device(): pl.pallas_call(functools.partial(exchange_kernel, bands, sky, epochs, sky...  18.5 us
    pallas_call x1, Pallas kernels, on_device(): pl.pallas_call(functools.partial(gather_kernel, sky), out_shape=jax.Shape...  13.6 us
    pallas_call x1, Pallas kernels, on_device(): pl.pallas_call(functools.partial(warp_kernel, bands, sky, epochs, rows),...  6.35 us
    unnamed x9, local copies, waits for them, and re-layouts  3.48 us

profile of v3, /device:TPU:14, one launch (start us, length us, event | category | flops | bytes accessed | tf_op | source)
XLA Modules:
  0.0 44.3 jit_solution(17231774916691696777)
XLA Ops:
  1.3 0.0 copy-start.2
  1.3 0.6 %copy-done.2 = bf16[6,2]{0,1:T(2,128)(2,1)S(1)} copy-done((bf16[6,2]{0,1:T(2,128)(2,1)S(1)}, bf16[6,2]{0,1:T(2,128)(2,1)}, u32[]{:S(2)}) %copy-start.2) | copy-done | bytes 48
  1.9 0.0 copy-start.1
  1.9 0.7 %copy-done.1 = bf16[6,3]{0,1:T(4,128)(2,1)S(1)} copy-done((bf16[6,3]{0,1:T(4,128)(2,1)S(1)}, bf16[6,3]{0,1:T(4,128)(2,1)}, u32[]{:S(2)}) %copy-start.1) | copy-done | bytes 60
  2.6 0.1 copy.14
  2.7 0.1 copy.13
  2.8 0.1 fusion.16
  3.0 0.1 reshape.24
  3.0 0.1 pad_maximum_fusion
  3.1 0.7 %copy.15.param_ref = f32[21,6]{1,0:T(8,128)} copy(f32[21,6]{0,1:T(8,128)S(1)} %pad_maximum_fusion) | data formatting | bytes 1008 | tf_op jit(solution)/shard_map/concatenate | solution.py:278
  3.8 13.6 %gather_templates.1.template_ref = bf16[4,3,32,512]{3,2,1,0:T(8,128)(2,1)} custom-call(bf16[3,32,512]{2,1,0:T(8,128)(2,1)} %template_ref.1), custom_call_target="tpu_custom_call" | custom-call | tf_op jit(solution)/shard_map/gather_templates/pallas_call | solution.py:262
  17.4 6.3 %warp_slots.1 = (bf16[8,3,32,256]{3,2,1,0:T(8,128)(2,1)}, f32[8,128]{1,0:T(8,128)}, f32[4,8,128]{2,1,0:T(8,128)}, bf16[8,4,8,256]{3,2,1,0:T(8,128)(2,1)}) custom-call(s32[6]{0:T(128)} %bitcast.15, s32[2,6]{1,0:T(2,128)} %bitcast.14, s32[1]{0:T(128)S(6)} %copy.18.count_ref, f32[21,6]{1,0:T(8,128)} %copy.15.param_ref, bf16[6,96,512]{2,1,0:T(8,128)(2,1)} %bitcast.13, ...), custom_call_target="tpu_custom_call" | custom-call | tf_op jit(solution)/shard_map/warp_slots/pallas_call | solution.py:285
  23.8 18.5 %exchange_sums.1 = (bf16[3,32,256]{2,1,0:T(8,128)(2,1)}, bf16[3,32,256]{2,1,0:T(8,128)(2,1)}) custom-call(bf16[8,3,32,256]{3,2,1,0:T(8,128)(2,1)} %get-tuple-element.7.send_ref, f32[8,128]{1,0:T(8,128)} %get-tuple-element.8.total_ref, f32[4,8,128]{2,1,0:T(8,128)} %get-tuple-element.9.rows_ref, bf16[8,4,8,256]{3,2,1,0:T(8,128)(2,1)} %get-tuple-element.10.cells_ref, ...), custom_call_target="tpu_custom_call" | custom-call | tf_op jit(solution)/shard_map/exchange_sums/pallas_call | solution.py:307
  42.2 0.0 copy-start
  42.3 1.4 %copy.19 = bf16[3,32,256]{2,1,0:T(8,128)(2,1)} copy(bf16[3,32,256]{2,1,0:T(8,128)(2,1)} %get-tuple-element.15) | data formatting | bytes 98304
  43.7 0.0 copy-done
  43.7 0.6 %copy.20 = bf16[3,32,256]{2,1,0:T(8,128)(2,1)} copy(bf16[3,32,256]{2,1,0:T(8,128)(2,1)S(1)} %copy-done) | data formatting | bytes 98304
  (4 shorter events, 0.0 us)
Async XLA Ops:
  1.3 0.7 %copy-start.2 = (bf16[6,2]{0,1:T(2,128)(2,1)S(1)}, bf16[6,2]{0,1:T(2,128)(2,1)}, u32[]{:S(2)}) copy-start(bf16[6,2]{0,1:T(2,128)(2,1)} %param.13) | copy-start | bytes 76
  1.9 0.7 %copy-start.1 = (bf16[6,3]{0,1:T(4,128)(2,1)S(1)}, bf16[6,3]{0,1:T(4,128)(2,1)}, u32[]{:S(2)}) copy-start(bf16[6,3]{0,1:T(4,128)(2,1)} %param.14) | copy-start | bytes 112
  42.2 1.4 %copy-start = (bf16[3,32,256]{2,1,0:T(8,128)(2,1)S(1)}, bf16[3,32,256]{2,1,0:T(8,128)(2,1)}, u32[]{:S(2)}) copy-start(bf16[3,32,256]{2,1,0:T(8,128)(2,1)} %get-tuple-element.16) | copy-start | bytes 147460
